TPU v7x, 32 devices: a whole 2x2x4 slice. The times are simulated.
32 devices in a mesh: reg: 4 (over y, core), prod: 8 (over z, x).
Axes of the slice: x: 2, y: 2, z: 4, core: 2. Of those that a mesh axis runs over, the one named last changes fastest.
Arguments:
- bottom_series_predictions: float32 [128, 256, 128], P('reg', 'prod'), may hold values from -6 to 6
- group_item_predictions: float32 [32, 256, 128], P('reg', 'prod'), may hold values from -18 to 18
- area_class_predictions: float32 [128, 32, 128], P('reg', 'prod'), may hold values from -18 to 18
- group_class_predictions: float32 [32, 32, 128], P('reg'), may hold values from -48 to 48
- bottom_series_precision: float32 [128, 256], P('reg', 'prod'), may hold values from 0.5 to 5
- group_item_precision: float32 [32, 256], P('reg', 'prod'), may hold values from 0.02 to 0.5
- area_class_precision: float32 [128, 32], P('reg', 'prod'), may hold values from 0.02 to 0.5
- group_class_precision: float32 [32, 32], P('reg'), may hold values from 0.002 to 0.05
- group_area_partition: int32 [32, 128], replicated, may hold values from -1 to 127, as said below
- class_item_partition: int32 [32, 128], replicated, may hold values from -1 to 255, as said below
Outputs:
- solution_field: float32 [128, 256, 128], P('reg', 'prod')
- residual: float32 [128, 256, 128], P('reg', 'prod')
Inputs may be any that keep to these rules, and one draw needn't show every extreme that they name: `group_area_partition`: every region stands in exactly one row; each row holds its parent's regions in its first slots and -1 in the rest; a parent has 1 to 97 regions, and some parent has exactly 97. `class_item_partition`: every product stands in exactly one row; each row holds its category's products in its first slots and -1 in the rest; a category has 1 to 128 products, and some category has exactly 128.
All inputs are finite; a program needn't handle non-finite values.
Results may differ from a plain program's by a relative error of at most 0.00011.
Values sent between devices are 32-bit elements; how exact they have to be, the bound alone decides.
A program may use at most 64 MiB of HBM per device.

v0:
```python
import jax
import jax.numpy as jnp
from jax import lax
from jax.sharding import PartitionSpec as P

ITERATIONS = 2


def member_local(table, first, count):
    items = first + jnp.arange(count, dtype=jnp.int32)
    return jnp.any(table[:, :, None] == items[None, None, :], axis=1).astype(jnp.float32)


def on_device(
    bottom_series_predictions,
    group_item_predictions,
    area_class_predictions,
    group_class_predictions,
    bottom_series_precision,
    group_item_precision,
    area_class_precision,
    group_class_precision,
    group_area_partition,
    class_item_partition,
):
    high = lax.Precision.HIGHEST
    areas_overall, items_overall, horizon_length = bottom_series_predictions.shape
    area_index_table = member_local(
        group_area_partition, lax.axis_index("reg") * areas_overall, areas_overall
    )
    item_index_table = member_local(
        class_item_partition, lax.axis_index("prod") * items_overall, items_overall
    )
    parent_share = area_index_table.shape[0] // lax.axis_size("reg")

    def disaggregate_onto(upper, lower):
        block = area_index_table
        total = jnp.einsum(
            "pr,pqh->rqh", block, lax.all_gather(upper, "reg", axis=0, tiled=True), precision=high
        )
        block = item_index_table
        return total + jnp.einsum(
            "crh,cq->rqh", lax.all_gather(lower, "prod", axis=0, tiled=True), block, precision=high
        )

    def replicate_across(corner):
        return jnp.einsum("pch,cq->pqh", corner, item_index_table, precision=high)

    def operate(field):
        rows_local = jnp.einsum("pr,rqh->pqh", area_index_table, field, precision=high)
        row_share = lax.psum_scatter(rows_local, "reg", scatter_dimension=0, tiled=True)
        col_share = lax.psum_scatter(
            jnp.einsum("cq,rqh->crh", item_index_table, field, precision=high),
            "prod",
            scatter_dimension=0,
            tiled=True,
        )
        partial_corner = jnp.einsum("pqh,cq->pch", rows_local, item_index_table, precision=high)
        whole = lax.psum(partial_corner, ("reg", "prod"))
        corner_share = lax.dynamic_slice_in_dim(
            whole, lax.axis_index("reg") * parent_share, parent_share, 0
        )
        upper = group_item_precision[:, :, None] * row_share + replicate_across(
            group_class_precision[:, :, None] * corner_share
        )
        lower = jnp.transpose(area_class_precision)[:, :, None] * col_share
        return bottom_series_precision[:, :, None] * field + disaggregate_onto(upper, lower)

    major_axis_first = group_item_precision[:, :, None] * group_item_predictions + replicate_across(
        group_class_precision[:, :, None] * group_class_predictions
    )
    lower_leading = jnp.transpose(
        area_class_precision[:, :, None] * area_class_predictions, (1, 0, 2)
    )
    system_source_term = bottom_series_precision[
        :, :, None
    ] * bottom_series_predictions + disaggregate_onto(major_axis_first, lower_leading)

    def two_products(vector, image):
        return lax.psum((jnp.sum(vector * vector), jnp.sum(vector * image)), ("reg", "prod"))

    solution_field = jnp.zeros_like(system_source_term)
    residual = system_source_term
    image = operate(residual)
    norm_now, product = two_products(residual, image)
    alpha = norm_now / product
    direction, along = (residual, image)
    for step in range(ITERATIONS):
        solution_field = solution_field + alpha * direction
        residual = residual - alpha * along
        if step + 1 < ITERATIONS:
            image = operate(residual)
            norm_next, product = two_products(residual, image)
            ratio = norm_next / norm_now
            alpha = norm_next / (product - ratio * norm_next / alpha)
            direction = residual + ratio * direction
            along = image + ratio * along
            norm_now = norm_next
    return (solution_field, residual)


def solution(mesh):
    return jax.shard_map(
        on_device,
        mesh=mesh,
        in_specs=(
            P("reg", "prod", None),
            P("reg", "prod", None),
            P("reg", "prod", None),
            P("reg", None, None),
            P("reg", "prod"),
            P("reg", "prod"),
            P("reg", "prod"),
            P("reg", None),
            P(),
            P(),
        ),
        out_specs=(P("reg", "prod", None), P("reg", "prod", None)),
        check_vma=False,
    )
```

profile of v0, /device:TPU:12, one launch (start us, length us, event | category | flops | bytes accessed | tf_op | source)
XLA Modules:
  0.0 496.7 jit_solution(14481580540045878076)
XLA Ops:
  10.1 1.3 fusion.5
  11.4 6.9 %all_gather.18 = f32[32,32,128]{2,1,0:T(8,128)S(1)} all-gather(f32[8,32,128]{2,1,0:T(8,128)S(1)} %fusion.5), channel_id=1, replica_groups=mesh['reg'=4,'prod'=8] {'reg'}, dimensions={0}, use_global_device_ids=true | all-gather | bytes 655360 | tf_op jit(solution)/shard_map/all_gather | solution.py:39
  18.4 29.1 %all_gather.19 = f32[32,32,128]{2,1,0:T(8,128)S(1)} all-gather(f32[4,32,128]{2,1,0:T(8,128)S(1)} %fusion.24), channel_id=1, replica_groups=mesh['reg'=4,'prod'=8] {'prod'}, dimensions={0}, use_global_device_ids=true | all-gather | bytes 589824 | tf_op jit(solution)/shard_map/all_gather | solution.py:43
  47.5 0.7 fusion.16
  48.2 0.7 compare_reduce_fusion.1
  48.9 1.3 fusion.2
  50.6 1.5 convolution_bitcast_fusion.1
  52.1 1.1 copy.80
  53.3 0.7 fusion.13
  54.1 1.1 copy.86
  55.2 129.7 %all-reduce.5.cloned.1.call-done = f32[32,32,128]{2,1,0:T(8,128)} async-done(((f32[32,32,128]{2,1,0:T(8,128)}), f32[32,32,128]{2,1,0:T(8,128)}) %all-reduce.5.cloned.1.call-update) | async-done | bytes 524304 | tf_op jit(solution)/shard_map/psum | solution.py:59
  184.9 1.3 fusion.4
  186.2 6.5 %all_gather.20 = f32[32,32,128]{2,1,0:T(8,128)S(1)} all-gather(f32[8,32,128]{2,1,0:T(8,128)S(1)} %fusion.4), channel_id=1, replica_groups=mesh['reg'=4,'prod'=8] {'reg'}, dimensions={0}, use_global_device_ids=true | all-gather | bytes 655360 | tf_op jit(solution)/shard_map/all_gather | solution.py:39
  192.7 0.9 broadcast_multiply_fusion.1
  193.6 28.7 %all_gather.21 = f32[32,32,128]{2,1,0:T(8,128)S(1)} all-gather(f32[4,32,128]{2,1,0:T(8,128)S(1)} %broadcast_multiply_fusion.1), channel_id=1, replica_groups=mesh['reg'=4,'prod'=8] {'prod'}, dimensions={0}, use_global_device_ids=true | all-gather | bytes 589824 | tf_op jit(solution)/shard_map/all_gather | solution.py:43
  222.3 0.7 fusion.11
  223.1 1.6 multiply_reduce_fusion.2
  224.7 43.1 %all-reduce.1 = (f32[]{:T(128)}, f32[]{:T(128)}) all-reduce(f32[]{:T(128)} %get-tuple-element.13, f32[]{:T(128)} %get-tuple-element.12), channel_id=1, replica_groups=mesh['reg'=4,'prod'=8] {'reg','prod'}, use_global_device_ids=true, to_apply=%region_3.0 | all-reduce | flops 2 | bytes 16 | tf_op jit(solution)/shard_map/psum | solution.py:80
  269.5 1.5 convolution_bitcast_fusion
  271.1 1.1 copy.90
  272.5 0.7 fusion.8
  273.2 1.1 copy.96
  274.3 125.1 %all-reduce.7.cloned.1.call-done = f32[32,32,128]{2,1,0:T(8,128)} async-done(((f32[32,32,128]{2,1,0:T(8,128)}), f32[32,32,128]{2,1,0:T(8,128)}) %all-reduce.7.cloned.1.call-update) | async-done | bytes 524304 | tf_op jit(solution)/shard_map/psum | solution.py:59
  399.4 1.3 fusion.3
  400.7 6.5 %all_gather.22 = f32[32,32,128]{2,1,0:T(8,128)S(1)} all-gather(f32[8,32,128]{2,1,0:T(8,128)S(1)} %fusion.3), channel_id=1, replica_groups=mesh['reg'=4,'prod'=8] {'reg'}, dimensions={0}, use_global_device_ids=true | all-gather | bytes 655360 | tf_op jit(solution)/shard_map/all_gather | solution.py:39
  407.2 0.9 broadcast_multiply_fusion
  408.1 28.8 %all_gather.23 = f32[32,32,128]{2,1,0:T(8,128)S(1)} all-gather(f32[4,32,128]{2,1,0:T(8,128)S(1)} %broadcast_multiply_fusion), channel_id=1, replica_groups=mesh['reg'=4,'prod'=8] {'prod'}, dimensions={0}, use_global_device_ids=true | all-gather | bytes 589824 | tf_op jit(solution)/shard_map/all_gather | solution.py:43
  436.9 0.7 fusion.6
  437.6 1.6 multiply_reduce_fusion
  439.2 42.9 %all-reduce = (f32[]{:T(128)}, f32[]{:T(128)}) all-reduce(f32[]{:T(128)} %get-tuple-element.11, f32[]{:T(128)} %get-tuple-element.10), channel_id=1, replica_groups=mesh['reg'=4,'prod'=8] {'reg','prod'}, use_global_device_ids=true, to_apply=%region_10.0 | all-reduce | flops 2 | bytes 16 | tf_op jit(solution)/shard_map/psum | solution.py:80
  486.9 1.1 copy.101
  488.0 1.1 copy.100
  (41 shorter events, 3.8 us)
Async XLA Ops:
  8.0 0.7 copy-start.5
  8.0 176.9 %all-reduce.5.cloned.1.call-start = ((), (), s32[]{:S(2)}) async-start(), calls=%async_computation.5 | async-start | bytes 1048576 | tf_op jit(solution)/shard_map/psum | solution.py:59
  8.7 0.7 copy-start.6
  9.4 0.7 copy-start.2
  9.4 0.7 copy-start.3
  11.4 6.9 %copy-start.1 = (f32[32,4,128]{2,1,0:T(4,128)S(1)}, f32[32,4,128]{2,1,0:T(4,128)}, u32[]{:S(2)}) copy-start(f32[32,4,128]{2,1,0:T(4,128)} %param.12) | copy-start | bytes 196612
  11.4 6.9 %copy-start.4 = (f32[32,4]{0,1:T(4,128)S(1)}, f32[32,4]{0,1:T(4,128)}, u32[]{:S(2)}) copy-start(f32[32,4]{0,1:T(4,128)} %param.16) | copy-start | bytes 1540
  47.5 0.7 copy-start.7
  47.5 1.4 copy-start
  52.1 132.8 %reduce-scatter.5.cloned.1.call-start = ((), (), s32[]{:S(2)}) async-start(), calls=%async_computation.4 | async-start | bytes 655360 | tf_op jit(solution)/shard_map/reduce_scatter | solution.py:51
  53.3 139.4 %reduce-scatter.7.cloned.1.call-start = ((), (), s32[]{:S(2)}) async-start(), calls=%async_computation.6 | async-start | bytes 589824 | tf_op jit(solution)/shard_map/reduce_scatter | solution.py:52
  55.2 344.2 %all-reduce.7.cloned.1.call-start = ((), (), s32[]{:S(2)}) async-start(), calls=%async_computation.8 | async-start | bytes 1048576 | tf_op jit(solution)/shard_map/psum | solution.py:59
  271.0 128.4 %reduce-scatter.9.cloned.1.call-start = ((), (), s32[]{:S(2)}) async-start(), calls=%async_computation.7 | async-start | bytes 655360 | tf_op jit(solution)/shard_map/reduce_scatter | solution.py:51
  272.2 134.9 %reduce-scatter.11.cloned.1.call-start = ((), (), s32[]{:S(2)}) async-start(), calls=%async_computation.9 | async-start | bytes 589824 | tf_op jit(solution)/shard_map/reduce_scatter | solution.py:52
Sparse Core Ops, SparseCore 0:
  52.2 132.6 all-reduce.4
  271.2 128.1 all-reduce.6
Sparse Core Ops, SparseCore 1:
  55.1 24.1 reduce-scatter.4
  83.0 63.4 reduce-scatter.6
  274.0 19.7 reduce-scatter.8
  297.7 63.5 reduce-scatter.10
where the time goes:
time: 498 us; the launch traced here: 497 us
  waiting for transfers between devices  255 us (51%)
  blocking collectives  192 us (39%)
  between operations  21.7 us (4%)
  matrix products  15.5 us (3%)
  local copies, waits for them, and re-layouts  8.02 us (2%)
    psum x2, waiting for transfers between devices, operate(): whole = lax.psum(partial_corner, ('reg', 'prod'))  255 us
    all_gather x3, blocking collectives, disaggregate_onto(): lax.all_gather(lower, 'prod', axis=0, tiled=True)  86.6 us
    psum x2, blocking collectives, two_products(): lax.psum((jnp.sum(vector * vector), jnp.sum(vector * image)), ('reg', 'pr...  86 us
    all_gather x3, blocking collectives, disaggregate_onto(): lax.all_gather(upper, 'reg', axis=0, tiled=True)  19.9 us
  transfers between devices with their start and end apart: 6, of which 2 were waited for; matrix products, arithmetic and copies ran while one was open for 2% of the time, Pallas kernels for 0%

commit v1 on v0

--- a/solution.py
+++ b/solution.py
@@ -56,7 +56,7 @@
             tiled=True,
         )
         partial_corner = jnp.einsum("pqh,cq->pch", rows_local, item_index_table, precision=high)
-        whole = lax.psum(partial_corner, ("reg", "prod"))
+        whole = jnp.sum(lax.all_gather(partial_corner, ("reg", "prod")), axis=0)
         corner_share = lax.dynamic_slice_in_dim(
             whole, lax.axis_index("reg") * parent_share, parent_share, 0
         )

time: 498 us -> 502 us (level)
  other arithmetic: 3.64 us -> 21.5 us
  waiting for transfers between devices: 255 us -> 240 us
    psum x2 -> x0, waiting for transfers between devices: 255 us -> none  [operate(): whole = lax.psum(partial_corner, ('reg', 'prod'))]
    reduce_scatter x2, waiting for transfers between devices: 0.01 us -> 240 us  [operate(): lax.psum_scatter(jnp.einsum('cq,rqh->crh', item_index_table, field, preci...]
    reduce_sum x0 -> x2, other arithmetic: none -> 15.6 us  [operate(): whole = jnp.sum(lax.all_gather(partial_corner, ('reg', 'prod')), axis=0)]
  transfers between devices with their start and end apart: 6 -> 6, of which waited for: 2 -> 2; matrix products, arithmetic and copies ran while one was open for 2% -> 5% of each run, Pallas kernels for 0% -> 0%
where the time goes in v1:
time: 502 us; the launch traced here: 501 us
  waiting for transfers between devices  240 us (48%)
  blocking collectives  194 us (39%)
  other arithmetic  21.5 us (4%)
  between operations  21.3 us (4%)
  matrix products  16.6 us (3%)
  local copies, waits for them, and re-layouts  7.41 us (1%)
    reduce_scatter x2, waiting for transfers between devices, operate(): lax.psum_scatter(jnp.einsum('cq,rqh->crh', item_index_table, field, preci...  240 us
    all_gather x3, blocking collectives, disaggregate_onto(): lax.all_gather(lower, 'prod', axis=0, tiled=True)  88.2 us
    psum x2, blocking collectives, two_products(): lax.psum((jnp.sum(vector * vector), jnp.sum(vector * image)), ('reg', 'pr...  85.9 us
    all_gather x3, blocking collectives, disaggregate_onto(): lax.all_gather(upper, 'reg', axis=0, tiled=True)  19.8 us
    reduce_sum x2, other arithmetic, operate(): whole = jnp.sum(lax.all_gather(partial_corner, ('reg', 'prod')), axis=0)  15.6 us
  transfers between devices with their start and end apart: 6, of which 2 were waited for; matrix products, arithmetic and copies ran while one was open for 5% of the time, Pallas kernels for 0%

profile of v1, /device:TPU:12, one launch (start us, length us, event | category | flops | bytes accessed | tf_op | source)
XLA Modules:
  0.0 500.6 jit_solution(6900620538386263515)
XLA Ops:
  8.1 0.8 copy.79
  8.9 1.4 compare_reduce_fusion
  10.3 1.3 fusion.5
  11.6 6.8 %all_gather.30 = f32[32,32,128]{2,1,0:T(8,128)S(1)} all-gather(f32[8,32,128]{2,1,0:T(8,128)S(1)} %fusion.5), channel_id=1, replica_groups=mesh['reg'=4,'prod'=8] {'reg'}, dimensions={0}, use_global_device_ids=true | all-gather | bytes 655360 | tf_op jit(solution)/shard_map/all_gather | solution.py:39
  18.4 0.9 fusion.24
  19.3 29.0 %all_gather.31 = f32[32,32,128]{2,1,0:T(8,128)S(1)} all-gather(f32[4,32,128]{2,1,0:T(8,128)S(1)} %fusion.24), channel_id=1, replica_groups=mesh['reg'=4,'prod'=8] {'prod'}, dimensions={0}, use_global_device_ids=true | all-gather | bytes 589824 | tf_op jit(solution)/shard_map/all_gather | solution.py:43
  49.1 1.4 compare_reduce_fusion.1
  50.5 2.4 fusion.2
  53.6 1.1 copy.94
  55.1 1.5 convolution_bitcast_fusion.1
  56.7 1.1 copy.88
  57.9 122.0 %reduce-scatter.7.cloned.1.call-done = f32[4,32,128]{2,1,0:T(8,128)} async-done(((f32[32,32,128]{2,1,0:T(8,128)}), f32[4,32,128]{2,1,0:T(8,128)}) %reduce-scatter.7.cloned.1.call-update) | async-done | bytes 65552 | tf_op jit(solution)/shard_map/reduce_scatter | solution.py:52
  179.9 0.9 broadcast_multiply_fusion.1
  180.8 29.6 %all_gather.35 = f32[32,32,128]{2,1,0:T(8,128)S(1)} all-gather(f32[4,32,128]{2,1,0:T(8,128)S(1)} %broadcast_multiply_fusion.1), channel_id=1, replica_groups=mesh['reg'=4,'prod'=8] {'prod'}, dimensions={0}, use_global_device_ids=true | all-gather | bytes 589824 | tf_op jit(solution)/shard_map/all_gather | solution.py:43
  211.1 7.8 %reduce_sum.55 = f32[32,32,128]{2,1,0:T(8,128)S(1)} reduce(f32[32,32,32,128]{3,2,1,0:T(8,128)} %bitcast.74, f32[]{:T(128)} %constant.6.clone.1), dimensions={0}, to_apply=%region_5.0 | reduce | flops 4063232 | bytes 17301508 | tf_op jit(solution)/shard_map/reduce_sum | solution.py:59
  219.0 1.2 fusion.4
  220.2 6.5 %all_gather.34 = f32[32,32,128]{2,1,0:T(8,128)S(1)} all-gather(f32[8,32,128]{2,1,0:T(8,128)S(1)} %fusion.4), channel_id=1, replica_groups=mesh['reg'=4,'prod'=8] {'reg'}, dimensions={0}, use_global_device_ids=true | all-gather | bytes 655360 | tf_op jit(solution)/shard_map/all_gather | solution.py:39
  226.7 1.6 multiply_reduce_fusion.2
  228.3 43.0 %all-reduce.1 = (f32[]{:T(128)}, f32[]{:T(128)}) all-reduce(f32[]{:T(128)} %get-tuple-element.13, f32[]{:T(128)} %get-tuple-element.12), channel_id=1, replica_groups=mesh['reg'=4,'prod'=8] {'reg','prod'}, use_global_device_ids=true, to_apply=%region_3.0 | all-reduce | flops 2 | bytes 16 | tf_op jit(solution)/shard_map/psum | solution.py:80
  273.4 1.1 copy.104
  275.0 1.5 convolution_bitcast_fusion
  276.5 1.1 copy.98
  277.7 117.6 %reduce-scatter.11.cloned.1.call-done = f32[4,32,128]{2,1,0:T(8,128)} async-done(((f32[32,32,128]{2,1,0:T(8,128)}), f32[4,32,128]{2,1,0:T(8,128)}) %reduce-scatter.11.cloned.1.call-update) | async-done | bytes 65552 | tf_op jit(solution)/shard_map/reduce_scatter | solution.py:52
  395.3 0.9 broadcast_multiply_fusion
  396.2 29.6 %all_gather.39 = f32[32,32,128]{2,1,0:T(8,128)S(1)} all-gather(f32[4,32,128]{2,1,0:T(8,128)S(1)} %broadcast_multiply_fusion), channel_id=1, replica_groups=mesh['reg'=4,'prod'=8] {'prod'}, dimensions={0}, use_global_device_ids=true | all-gather | bytes 589824 | tf_op jit(solution)/shard_map/all_gather | solution.py:43
  426.6 7.8 %reduce_sum.58 = f32[32,32,128]{2,1,0:T(8,128)S(1)} reduce(f32[32,32,32,128]{3,2,1,0:T(8,128)} %bitcast.75, f32[]{:T(128)} %constant.6.clone.1), dimensions={0}, to_apply=%region_12.0 | reduce | flops 4063232 | bytes 17301508 | tf_op jit(solution)/shard_map/reduce_sum | solution.py:59
  434.4 1.2 fusion.3
  435.6 6.5 %all_gather.38 = f32[32,32,128]{2,1,0:T(8,128)S(1)} all-gather(f32[8,32,128]{2,1,0:T(8,128)S(1)} %fusion.3), channel_id=1, replica_groups=mesh['reg'=4,'prod'=8] {'reg'}, dimensions={0}, use_global_device_ids=true | all-gather | bytes 655360 | tf_op jit(solution)/shard_map/all_gather | solution.py:39
  442.1 1.6 multiply_reduce_fusion
  443.7 42.8 %all-reduce = (f32[]{:T(128)}, f32[]{:T(128)}) all-reduce(f32[]{:T(128)} %get-tuple-element.11, f32[]{:T(128)} %get-tuple-element.10), channel_id=1, replica_groups=mesh['reg'=4,'prod'=8] {'reg','prod'}, use_global_device_ids=true, to_apply=%region_10.0 | all-reduce | flops 2 | bytes 16 | tf_op jit(solution)/shard_map/psum | solution.py:80
  491.3 1.1 copy.109
  492.4 1.1 copy.108
  (33 shorter events, 5.1 us)
Async XLA Ops:
  8.0 210.9 %copy-start = (f32[8,32]{1,0:T(8,128)S(1)}, f32[8,32]{1,0:T(8,128)}, u32[]{:S(2)}) copy-start(f32[8,32]{1,0:T(8,128)} %param.17) | copy-start | bytes 3076
  8.0 210.9 %copy-start.1 = (f32[8,32]{1,0:T(8,128)S(1)}, f32[8,32]{1,0:T(8,128)}, u32[]{:S(2)}) copy-start(f32[8,32]{1,0:T(8,128)} %param.15) | copy-start | bytes 3076
  8.0 171.9 %reduce-scatter.7.cloned.1.call-start = ((), (), s32[]{:S(2)}) async-start(), calls=%async_computation.5 | async-start | bytes 589824 | tf_op jit(solution)/shard_map/reduce_scatter | solution.py:52
  54.7 156.4 %all-gather.5.cloned.1.call-start = ((), (), s32[]{:S(2)}) async-start(), calls=%async_computation.8 | async-start | bytes 17301504 | tf_op jit(solution)/shard_map/all_gather | solution.py:59
  55.1 340.2 %copy-start.2 = (f32[32,4]{0,1:T(4,128)S(1)}, f32[32,4]{0,1:T(4,128)}, u32[]{:S(2)}) copy-start(f32[32,4]{0,1:T(4,128)} %param.16) | copy-start | bytes 1540
  56.7 162.3 %reduce-scatter.5.cloned.1.call-start = ((), (), s32[]{:S(2)}) async-start(), calls=%async_computation.4 | async-start | bytes 655360 | tf_op jit(solution)/shard_map/reduce_scatter | solution.py:51
  57.8 337.4 %reduce-scatter.11.cloned.1.call-start = ((), (), s32[]{:S(2)}) async-start(), calls=%async_computation.7 | async-start | bytes 589824 | tf_op jit(solution)/shard_map/reduce_scatter | solution.py:52
  274.5 152.0 %all-gather.7.cloned.1.call-start = ((), (), s32[]{:S(2)}) async-start(), calls=%async_computation.9 | async-start | bytes 17301504 | tf_op jit(solution)/shard_map/all_gather | solution.py:59
  276.5 157.9 %reduce-scatter.9.cloned.1.call-start = ((), (), s32[]{:S(2)}) async-start(), calls=%async_computation.6 | async-start | bytes 655360 | tf_op jit(solution)/shard_map/reduce_scatter | solution.py:51
Sparse Core Ops, SparseCore 0:
  54.8 125.0 reduce-scatter.6
  182.4 20.6 reduce-scatter.4
  274.6 120.5 reduce-scatter.10
  397.6 20.6 reduce-scatter.8
Sparse Core Ops, SparseCore 1:
  58.7 118.9 all-gather.4
  278.6 114.5 all-gather.6
